TPU v7x, 32 devices: a whole 2x2x4 slice. The times are simulated.
32 devices in a mesh: occ: 8 (over z, y), ao: 4 (over x, core).
Axes of the slice: x: 2, y: 2, z: 4, core: 2. Of those that a mesh axis runs over, the one named last changes fastest.
Arguments:
- amplitudes: bfloat16 [8, 640, 19456], P(None, 'occ', 'ao'), may hold values from -6 to 6
- occ_coef: bfloat16 [512, 640], P(None, 'occ'), may hold values from -0.25 to 0.25
- vir_coef: bfloat16 [512, 19456], P('occ', 'ao'), may hold values from -0.25 to 0.25
- occ_energy: float32 [640], P('occ'), may hold values from -1.5 to -0.3
- vir_energy: float32 [19456], P('ao'), may hold values from 0.05 to 2.5
- kernel: float32 [512], replicated, may hold values from 2 to 10
Outputs:
- residual: bfloat16 [8, 640, 19456], P(None, 'occ', 'ao')
- projected: float32 [8, 8], replicated
All inputs are finite; a program needn't handle non-finite values.
Results may differ from a plain program's by a relative error of at most 0.0049.
Values may be sent and summed in bfloat16 or wider, within the bound.
A program may use at most 128 MiB of HBM per device.

v0:
```python
import jax
import jax.numpy as jnp
from jax import lax
from jax.sharding import PartitionSpec as P


def shards(amplitudes, occ_coef, vir_coef, occ_energy, vir_energy, kernel):
    trials, occ_dev, vir_dev = amplitudes.shape
    row_total = occ_coef.shape[0]
    flat_amps = amplitudes.reshape(trials * occ_dev, vir_dev)
    occ_trans = occ_coef.T.astype(jnp.float32)
    whole_rows = lax.all_gather(vir_coef, "occ", axis=0, tiled=True)
    row_count = whole_rows.shape[0]
    half_done = lax.dot_general(
        flat_amps, whole_rows, (((1,), (1,)), ((), ())), preferred_element_type=jnp.float32
    )
    half_done = half_done.reshape(trials, occ_dev, row_count)
    partial_value = jnp.sum(half_done * occ_trans[None], axis=1)
    amps_rows = amplitudes.reshape(trials, occ_dev * vir_dev)
    density = lax.psum(partial_value, ("occ", "ao"))
    potential = kernel[None, :] * density
    weighted = (
        (occ_trans[None] * potential[:, None, :])
        .astype(jnp.bfloat16)
        .reshape(trials * occ_dev, row_total)
    )
    coupling = jnp.dot(weighted, whole_rows, preferred_element_type=jnp.float32)
    energy_gaps = vir_energy[None, :] - occ_energy[:, None]
    sigma_block = energy_gaps[None] * amplitudes.astype(jnp.float32) + coupling.reshape(
        trials, occ_dev, vir_dev
    )

    def gram_column(sigma_one):
        return jnp.sum(amplitudes.astype(jnp.float32) * sigma_one[None], axis=(1, 2))

    gram_local = lax.map(gram_column, sigma_block).T
    correlation_local = jnp.dot(amps_rows, amps_rows.T, preferred_element_type=jnp.float32)
    gram, correlation = lax.psum((gram_local, correlation_local), ("occ", "ao"))
    norms = jnp.diagonal(correlation) + 1e-06
    ritz_values = jnp.diagonal(gram) / norms
    residual = (sigma_block - ritz_values[:, None, None] * amplitudes.astype(jnp.float32)).astype(
        jnp.bfloat16
    )
    projected = gram / jnp.sqrt(norms[:, None] * norms[None, :])
    return (residual, projected)


def solution(mesh):
    placed = (P(None, "occ", "ao"), P(None, "occ"), P("occ", "ao"), P("occ"), P("ao"), P())
    return jax.shard_map(
        shards, mesh=mesh, in_specs=placed, out_specs=(P(None, "occ", "ao"), P()), check_vma=False
    )
```

profile of v0, /device:TPU:0, one launch (start us, length us, event | category | flops | bytes accessed | tf_op | source)
XLA Modules:
  0.0 258.6 jit_solution(4018655278099293986)
XLA Ops:
  8.8 11.1 %fusion.14 = f32[8,8]{1,0:T(8,128)S(1)} fusion(bf16[8,80,4864]{2,1,0:T(8,128)(2,1)} %param.8), kind=kOutput, calls=%fused_computation.17 | convolution fusion | flops 49807360 | bytes 6226176 | tf_op jit(solution)/shard_map/dot_general | solution.py:37
  20.1 75.4 %all-gather.2.cloned.1.call-done = bf16[512,4864]{1,0:T(8,128)(2,1)} async-done(((bf16[64,4864]{1,0:T(8,128)(2,1)}), bf16[512,4864]{1,0:T(8,128)(2,1)}) %all-gather.2.cloned.1.call-update) | async-done | bytes 4980752 | tf_op jit(solution)/shard_map/all_gather | solution.py:12
  95.5 7.6 %fusion.11 = f32[8,512]{1,0:T(8,128)S(1)} fusion(bf16[8,80,4864]{2,1,0:T(8,128)(2,1)} %param.8, bf16[512,4864]{1,0:T(8,128)(2,1)} %all-gather.2.cloned.1.call-done, f32[80,512]{1,0:T(8,128)S(1)} %convert_bitcast_fusion), kind=kOutput, calls=%fused_computation.16 | convolution fusion | flops 3188322304 | bytes 11386880 | tf_op jit(solution)/shard_map/dot_general | solution.py:14
  103.2 38.8 %psum.21 = f32[8,512]{1,0:T(8,128)S(1)} all-reduce(f32[8,512]{1,0:T(8,128)S(1)} %fusion.11), channel_id=1, replica_groups=mesh['occ'=8,'ao'=4] {'occ','ao'}, use_global_device_ids=true, to_apply=%region_1.0 | all-reduce | flops 4096 | bytes 32768 | tf_op jit(solution)/shard_map/psum | solution.py:20
  142.0 9.7 %fusion = f32[8,80,4864]{2,1,0:T(8,128)} fusion(bf16[8,80,4864]{2,1,0:T(8,128)(2,1)} %param.8, f32[80,4864]{1,0:T(8,128)S(1)} %broadcast_subtract_fusion, bf16[512,4864]{1,0:T(8,128)(2,1)} %all-gather.2.cloned.1.call-done, f32[8,512]{1,0:T(8,128)S(1)} %broadcast_multiply_fusion, f32[80,512]{1,0:T(8,128)S(1)} %convert_bitcast_fusion), kind=kOutput, calls=%fused_computation.6 | convolution fusion | flops 3197665280 | bytes 25395200 | tf_op jit(solution)/shard_map/dot_general | solution.py:27
  151.7 46.7 %while.10 = (s32[]{:T(128)}, f32[8,8]{1,0:T(8,128)S(1)}, bf16[8,80,4864]{2,1,0:T(8,128)(2,1)}, f32[8,80,4864]{2,1,0:T(8,128)}, s32[]{:T(128)}, /*index=5*/s32[]{:T(128)}) while((s32[]{:T(128)}, f32[8,8]{1,0:T(8,128)S(1)}, bf16[8,80,4864]{2,1,0:T(8,128)(2,1)}, f32[8,80,4864]{2,1,0:T(8,128)}, s32[]{:T(128)}, /*index=5*/s32[]{:T(128)}) %tuple.23), condition=%wide.region_4.5_spmd, body=%wide.region_2.4_spmd.sunk | while | flops 9338874 | bytes 10895533 | solution.py:36
  151.7 1.5 dynamic-slice_bitcast_fusion.2
  153.2 4.3 %multiply_reduce_fusion.2 = f32[8]{0:T(128)S(1)} fusion(bf16[8,80,4864]{2,1,0:T(8,128)(2,1)} %get-tuple-element.76, f32[80,4864]{1,0:T(8,128)S(1)} %dynamic-slice_bitcast_fusion.2), kind=kLoop, calls=%fused_computation.2.clone.1 | loop fusion | flops 9338872 | bytes 7782432 | tf_op jit(solution)/shard_map/while/body/eval_jaxpr/reduce_sum | solution.py:34
  157.5 1.5 dynamic-slice_bitcast_fusion.2
  159.0 4.3 %multiply_reduce_fusion.2 = f32[8]{0:T(128)S(1)} fusion(bf16[8,80,4864]{2,1,0:T(8,128)(2,1)} %get-tuple-element.76, f32[80,4864]{1,0:T(8,128)S(1)} %dynamic-slice_bitcast_fusion.2), kind=kLoop, calls=%fused_computation.2.clone.1 | loop fusion | flops 9338872 | bytes 7782432 | tf_op jit(solution)/shard_map/while/body/eval_jaxpr/reduce_sum | solution.py:34
  163.3 1.5 dynamic-slice_bitcast_fusion.2
  164.8 4.3 %multiply_reduce_fusion.2 = f32[8]{0:T(128)S(1)} fusion(bf16[8,80,4864]{2,1,0:T(8,128)(2,1)} %get-tuple-element.76, f32[80,4864]{1,0:T(8,128)S(1)} %dynamic-slice_bitcast_fusion.2), kind=kLoop, calls=%fused_computation.2.clone.1 | loop fusion | flops 9338872 | bytes 7782432 | tf_op jit(solution)/shard_map/while/body/eval_jaxpr/reduce_sum | solution.py:34
  169.2 1.5 dynamic-slice_bitcast_fusion.2
  170.7 4.3 %multiply_reduce_fusion.2 = f32[8]{0:T(128)S(1)} fusion(bf16[8,80,4864]{2,1,0:T(8,128)(2,1)} %get-tuple-element.76, f32[80,4864]{1,0:T(8,128)S(1)} %dynamic-slice_bitcast_fusion.2), kind=kLoop, calls=%fused_computation.2.clone.1 | loop fusion | flops 9338872 | bytes 7782432 | tf_op jit(solution)/shard_map/while/body/eval_jaxpr/reduce_sum | solution.py:34
  175.0 1.5 dynamic-slice_bitcast_fusion.2
  176.5 4.3 %multiply_reduce_fusion.2 = f32[8]{0:T(128)S(1)} fusion(bf16[8,80,4864]{2,1,0:T(8,128)(2,1)} %get-tuple-element.76, f32[80,4864]{1,0:T(8,128)S(1)} %dynamic-slice_bitcast_fusion.2), kind=kLoop, calls=%fused_computation.2.clone.1 | loop fusion | flops 9338872 | bytes 7782432 | tf_op jit(solution)/shard_map/while/body/eval_jaxpr/reduce_sum | solution.py:34
  180.8 1.5 dynamic-slice_bitcast_fusion.2
  182.3 4.3 %multiply_reduce_fusion.2 = f32[8]{0:T(128)S(1)} fusion(bf16[8,80,4864]{2,1,0:T(8,128)(2,1)} %get-tuple-element.76, f32[80,4864]{1,0:T(8,128)S(1)} %dynamic-slice_bitcast_fusion.2), kind=kLoop, calls=%fused_computation.2.clone.1 | loop fusion | flops 9338872 | bytes 7782432 | tf_op jit(solution)/shard_map/while/body/eval_jaxpr/reduce_sum | solution.py:34
  186.7 1.5 dynamic-slice_bitcast_fusion.2
  188.2 4.3 %multiply_reduce_fusion.2 = f32[8]{0:T(128)S(1)} fusion(bf16[8,80,4864]{2,1,0:T(8,128)(2,1)} %get-tuple-element.76, f32[80,4864]{1,0:T(8,128)S(1)} %dynamic-slice_bitcast_fusion.2), kind=kLoop, calls=%fused_computation.2.clone.1 | loop fusion | flops 9338872 | bytes 7782432 | tf_op jit(solution)/shard_map/while/body/eval_jaxpr/reduce_sum | solution.py:34
  192.5 1.5 dynamic-slice_bitcast_fusion.2
  194.0 4.3 %multiply_reduce_fusion.2 = f32[8]{0:T(128)S(1)} fusion(bf16[8,80,4864]{2,1,0:T(8,128)(2,1)} %get-tuple-element.76, f32[80,4864]{1,0:T(8,128)S(1)} %dynamic-slice_bitcast_fusion.2), kind=kLoop, calls=%fused_computation.2.clone.1 | loop fusion | flops 9338872 | bytes 7782432 | tf_op jit(solution)/shard_map/while/body/eval_jaxpr/reduce_sum | solution.py:34
  198.4 40.7 %all-reduce = (f32[8,8]{1,0:T(8,128)S(1)}, f32[8,8]{1,0:T(8,128)S(1)}) all-reduce(f32[8,8]{1,0:T(8,128)S(1)} %bitcast.25, f32[8,8]{1,0:T(8,128)S(1)} %fusion.14), channel_id=1, replica_groups=mesh['occ'=8,'ao'=4] {'occ','ao'}, use_global_device_ids=true, to_apply=%region_5.6 | all-reduce | flops 128 | bytes 1024 | tf_op jit(solution)/shard_map/psum | solution.py:38
  241.0 10.8 %fusion.2 = bf16[8,80,4864]{2,1,0:T(8,128)(2,1)} fusion(f32[8,80,4864]{2,1,0:T(8,128)} %get-tuple-element.82, bf16[8,80,4864]{2,1,0:T(8,128)(2,1)} %get-tuple-element.81, f32[8]{0:T(128)S(1)} %get-tuple-element.36), kind=kLoop, calls=%fused_computation.8 | loop fusion | flops 12451840 | bytes 24903712 | tf_op jit(solution)/shard_map/convert_element_type | solution.py:41
  (26 shorter events, 4.0 us)
Async XLA Ops:
  7.2 12.8 %copy-start.2 = (f32[80]{0:T(128)S(1)}, f32[80]{0:T(128)}, u32[]{:S(2)}) copy-start(f32[80]{0:T(128)} %param.11) | copy-start | bytes 964
  7.2 12.8 %copy-start = (f32[4864]{0:T(1024)S(1)}, f32[4864]{0:T(1024)}, u32[]{:S(2)}) copy-start(f32[4864]{0:T(1024)} %param.12) | copy-start | bytes 58372
  7.2 88.4 %all-gather.2.cloned.1.call-start = ((), (), s32[]{:S(2)}) async-start(), calls=%async_computation | async-start | bytes 5603328 | tf_op jit(solution)/shard_map/all_gather | solution.py:12
  20.1 121.8 %copy-start.1 = (f32[512]{0:T(512)S(1)}, f32[512]{0:T(512)}, u32[]{:S(2)}) copy-start(f32[512]{0:T(512)} %param.13) | copy-start | bytes 6148
Sparse Core Ops, SparseCore 0:
  10.2 85.3 all-gather.1
where the time goes:
time: 259 us
  blocking collectives  79.5 us (31%)
  waiting for transfers between devices  76.1 us (29%)
  other arithmetic  46.9 us (18%)
  matrix products  28.4 us (11%)
  between operations  14.1 us (5%)
  local copies, waits for them, and re-layouts  13.6 us (5%)
    all_gather x1, waiting for transfers between devices, shards(): whole_rows = lax.all_gather(vir_coef, 'occ', axis=0, tiled=True)  75.4 us
    psum x1, blocking collectives, shards(): gram, correlation = lax.psum((gram_local, correlation_local), ('occ', 'ao'))  40.7 us
    psum x1, blocking collectives, shards(): density = lax.psum(partial_value, ('occ', 'ao'))  38.8 us
    reduce_sum x8, other arithmetic, gram_column(): jnp.sum(amplitudes.astype(jnp.float32) * sigma_one[None], axis=(1, 2))  34.4 us
    mul x8, local copies, waits for them, and re-layouts, gram_column(): amplitudes.astype(jnp.float32) * sigma_one[None]  12.1 us
    dot_general x1, matrix products, shards(): jnp.dot(amps_rows, amps_rows.T, preferred_element_type=jnp.float32)  11.1 us
    convert_element_type x1, other arithmetic, shards(): (sigma_block - ritz_values[:, None, None] * amplitudes.astype(jnp.float32...  10.8 us
    dot_general x1, matrix products, shards(): coupling = jnp.dot(weighted, whole_rows, preferred_element_type=jnp.float32)  9.7 us
  transfers between devices with their start and end apart: 1, of which 1 were waited for; matrix products, arithmetic and copies ran while one was open for 5% of the time, Pallas kernels for 0%

commit v1 on v0

--- a/solution.py
+++ b/solution.py
@@ -17,7 +17,8 @@
     half_done = half_done.reshape(trials, occ_dev, row_count)
     partial_value = jnp.sum(half_done * occ_trans[None], axis=1)
     amps_rows = amplitudes.reshape(trials, occ_dev * vir_dev)
-    density = lax.psum(partial_value, ("occ", "ao"))
+    one_axis = lax.psum(partial_value, "ao")
+    density = lax.psum(one_axis, "occ")
     potential = kernel[None, :] * density
     weighted = (
         (occ_trans[None] * potential[:, None, :])

time: 259 us -> 263 us (1.015)
  blocking collectives: 79.5 us -> 82.5 us
    psum x1 -> x2, blocking collectives: 38.8 us -> 45.6 us  [the longest x1 35.5 us: shards(): density = lax.psum(one_axis, 'occ')]
    psum x1, blocking collectives: 40.7 us -> 36.9 us  [shards(): gram, correlation = lax.psum((gram_local, correlation_local), ('occ', 'ao'))]
where the time goes in v1:
time: 263 us; the launch traced here: 262 us
  blocking collectives  82.5 us (31%)
  waiting for transfers between devices  76.1 us (29%)
  other arithmetic  46.9 us (18%)
  matrix products  28.4 us (11%)
  between operations  14.1 us (5%)
  local copies, waits for them, and re-layouts  13.6 us (5%)
    all_gather x1, waiting for transfers between devices, shards(): whole_rows = lax.all_gather(vir_coef, 'occ', axis=0, tiled=True)  75.4 us
    psum x1, blocking collectives, shards(): gram, correlation = lax.psum((gram_local, correlation_local), ('occ', 'ao'))  36.9 us
    psum x1, blocking collectives, shards(): density = lax.psum(one_axis, 'occ')  35.5 us
    reduce_sum x8, other arithmetic, gram_column(): jnp.sum(amplitudes.astype(jnp.float32) * sigma_one[None], axis=(1, 2))  34.4 us
    mul x8, local copies, waits for them, and re-layouts, gram_column(): amplitudes.astype(jnp.float32) * sigma_one[None]  12.1 us
    dot_general x1, matrix products, shards(): jnp.dot(amps_rows, amps_rows.T, preferred_element_type=jnp.float32)  11.1 us
    convert_element_type x1, other arithmetic, shards(): (sigma_block - ritz_values[:, None, None] * amplitudes.astype(jnp.float32...  10.8 us
    psum x1, blocking collectives, shards(): one_axis = lax.psum(partial_value, 'ao')  10.1 us
  transfers between devices with their start and end apart: 1, of which 1 were waited for; matrix products, arithmetic and copies ran while one was open for 5% of the time, Pallas kernels for 0%

profile of v1, /device:TPU:0, one launch (start us, length us, event | category | flops | bytes accessed | tf_op | source)
XLA Modules:
  0.0 261.6 jit_solution(8905115315609625792)
XLA Ops:
  8.8 11.1 %fusion.14 = f32[8,8]{1,0:T(8,128)S(1)} fusion(bf16[8,80,4864]{2,1,0:T(8,128)(2,1)} %param.8), kind=kOutput, calls=%fused_computation.17 | convolution fusion | flops 49807360 | bytes 6226176 | tf_op jit(solution)/shard_map/dot_general | solution.py:38
  20.1 75.4 %all-gather.2.cloned.1.call-done = bf16[512,4864]{1,0:T(8,128)(2,1)} async-done(((bf16[64,4864]{1,0:T(8,128)(2,1)}), bf16[512,4864]{1,0:T(8,128)(2,1)}) %all-gather.2.cloned.1.call-update) | async-done | bytes 4980752 | tf_op jit(solution)/shard_map/all_gather | solution.py:12
  95.5 7.6 %fusion.11 = f32[8,512]{1,0:T(8,128)S(1)} fusion(bf16[8,80,4864]{2,1,0:T(8,128)(2,1)} %param.8, bf16[512,4864]{1,0:T(8,128)(2,1)} %all-gather.2.cloned.1.call-done, f32[80,512]{1,0:T(8,128)S(1)} %convert_bitcast_fusion), kind=kOutput, calls=%fused_computation.16 | convolution fusion | flops 3188322304 | bytes 11386880 | tf_op jit(solution)/shard_map/dot_general | solution.py:14
  103.2 10.1 %psum.28 = f32[8,512]{1,0:T(8,128)S(1)} all-reduce(f32[8,512]{1,0:T(8,128)S(1)} %fusion.11), channel_id=1, replica_groups=mesh['occ'=8,'ao'=4] {'ao'}, use_global_device_ids=true, to_apply=%region_1.0 | all-reduce | flops 4096 | bytes 32768 | tf_op jit(solution)/shard_map/psum | solution.py:20
  113.3 35.5 %psum.29 = f32[8,512]{1,0:T(8,128)S(1)} all-reduce(f32[8,512]{1,0:T(8,128)S(1)} %psum.28), channel_id=1, replica_groups=mesh['occ'=8,'ao'=4] {'occ'}, use_global_device_ids=true, to_apply=%region_2.0 | all-reduce | flops 4096 | bytes 32768 | tf_op jit(solution)/shard_map/psum | solution.py:21
  148.8 9.7 %fusion = f32[8,80,4864]{2,1,0:T(8,128)} fusion(bf16[8,80,4864]{2,1,0:T(8,128)(2,1)} %param.8, f32[80,4864]{1,0:T(8,128)S(1)} %broadcast_subtract_fusion, bf16[512,4864]{1,0:T(8,128)(2,1)} %all-gather.2.cloned.1.call-done, f32[8,512]{1,0:T(8,128)S(1)} %broadcast_multiply_fusion, f32[80,512]{1,0:T(8,128)S(1)} %convert_bitcast_fusion), kind=kOutput, calls=%fused_computation.6 | convolution fusion | flops 3197665280 | bytes 25395200 | tf_op jit(solution)/shard_map/dot_general | solution.py:28
  158.5 46.7 %while.10 = (s32[]{:T(128)}, f32[8,8]{1,0:T(8,128)S(1)}, bf16[8,80,4864]{2,1,0:T(8,128)(2,1)}, f32[8,80,4864]{2,1,0:T(8,128)}, s32[]{:T(128)}, /*index=5*/s32[]{:T(128)}) while((s32[]{:T(128)}, f32[8,8]{1,0:T(8,128)S(1)}, bf16[8,80,4864]{2,1,0:T(8,128)(2,1)}, f32[8,80,4864]{2,1,0:T(8,128)}, s32[]{:T(128)}, /*index=5*/s32[]{:T(128)}) %tuple.23), condition=%wide.region_5.6_spmd, body=%wide.region_3.5_spmd.sunk | while | flops 9338874 | bytes 10895533 | solution.py:37
  160.0 4.3 %multiply_reduce_fusion.2 = f32[8]{0:T(128)S(1)} fusion(bf16[8,80,4864]{2,1,0:T(8,128)(2,1)} %get-tuple-element.76, f32[80,4864]{1,0:T(8,128)S(1)} %dynamic-slice_bitcast_fusion.2), kind=kLoop, calls=%fused_computation.2.clone.1 | loop fusion | flops 9338872 | bytes 7782432 | tf_op jit(solution)/shard_map/while/body/eval_jaxpr/reduce_sum | solution.py:35
  164.3 1.5 dynamic-slice_bitcast_fusion.2
  165.8 4.3 %multiply_reduce_fusion.2 = f32[8]{0:T(128)S(1)} fusion(bf16[8,80,4864]{2,1,0:T(8,128)(2,1)} %get-tuple-element.76, f32[80,4864]{1,0:T(8,128)S(1)} %dynamic-slice_bitcast_fusion.2), kind=kLoop, calls=%fused_computation.2.clone.1 | loop fusion | flops 9338872 | bytes 7782432 | tf_op jit(solution)/shard_map/while/body/eval_jaxpr/reduce_sum | solution.py:35
  170.1 1.5 dynamic-slice_bitcast_fusion.2
  171.6 4.3 %multiply_reduce_fusion.2 = f32[8]{0:T(128)S(1)} fusion(bf16[8,80,4864]{2,1,0:T(8,128)(2,1)} %get-tuple-element.76, f32[80,4864]{1,0:T(8,128)S(1)} %dynamic-slice_bitcast_fusion.2), kind=kLoop, calls=%fused_computation.2.clone.1 | loop fusion | flops 9338872 | bytes 7782432 | tf_op jit(solution)/shard_map/while/body/eval_jaxpr/reduce_sum | solution.py:35
  176.0 1.5 dynamic-slice_bitcast_fusion.2
  177.5 4.3 %multiply_reduce_fusion.2 = f32[8]{0:T(128)S(1)} fusion(bf16[8,80,4864]{2,1,0:T(8,128)(2,1)} %get-tuple-element.76, f32[80,4864]{1,0:T(8,128)S(1)} %dynamic-slice_bitcast_fusion.2), kind=kLoop, calls=%fused_computation.2.clone.1 | loop fusion | flops 9338872 | bytes 7782432 | tf_op jit(solution)/shard_map/while/body/eval_jaxpr/reduce_sum | solution.py:35
  181.8 1.5 dynamic-slice_bitcast_fusion.2
  183.3 4.3 %multiply_reduce_fusion.2 = f32[8]{0:T(128)S(1)} fusion(bf16[8,80,4864]{2,1,0:T(8,128)(2,1)} %get-tuple-element.76, f32[80,4864]{1,0:T(8,128)S(1)} %dynamic-slice_bitcast_fusion.2), kind=kLoop, calls=%fused_computation.2.clone.1 | loop fusion | flops 9338872 | bytes 7782432 | tf_op jit(solution)/shard_map/while/body/eval_jaxpr/reduce_sum | solution.py:35
  187.6 1.5 dynamic-slice_bitcast_fusion.2
  189.1 4.3 %multiply_reduce_fusion.2 = f32[8]{0:T(128)S(1)} fusion(bf16[8,80,4864]{2,1,0:T(8,128)(2,1)} %get-tuple-element.76, f32[80,4864]{1,0:T(8,128)S(1)} %dynamic-slice_bitcast_fusion.2), kind=kLoop, calls=%fused_computation.2.clone.1 | loop fusion | flops 9338872 | bytes 7782432 | tf_op jit(solution)/shard_map/while/body/eval_jaxpr/reduce_sum | solution.py:35
  193.5 1.5 dynamic-slice_bitcast_fusion.2
  195.0 4.3 %multiply_reduce_fusion.2 = f32[8]{0:T(128)S(1)} fusion(bf16[8,80,4864]{2,1,0:T(8,128)(2,1)} %get-tuple-element.76, f32[80,4864]{1,0:T(8,128)S(1)} %dynamic-slice_bitcast_fusion.2), kind=kLoop, calls=%fused_computation.2.clone.1 | loop fusion | flops 9338872 | bytes 7782432 | tf_op jit(solution)/shard_map/while/body/eval_jaxpr/reduce_sum | solution.py:35
  199.3 1.5 dynamic-slice_bitcast_fusion.2
  200.8 4.3 %multiply_reduce_fusion.2 = f32[8]{0:T(128)S(1)} fusion(bf16[8,80,4864]{2,1,0:T(8,128)(2,1)} %get-tuple-element.76, f32[80,4864]{1,0:T(8,128)S(1)} %dynamic-slice_bitcast_fusion.2), kind=kLoop, calls=%fused_computation.2.clone.1 | loop fusion | flops 9338872 | bytes 7782432 | tf_op jit(solution)/shard_map/while/body/eval_jaxpr/reduce_sum | solution.py:35
  205.2 36.9 %all-reduce = (f32[8,8]{1,0:T(8,128)S(1)}, f32[8,8]{1,0:T(8,128)S(1)}) all-reduce(f32[8,8]{1,0:T(8,128)S(1)} %bitcast.25, f32[8,8]{1,0:T(8,128)S(1)} %fusion.14), channel_id=1, replica_groups=mesh['occ'=8,'ao'=4] {'occ','ao'}, use_global_device_ids=true, to_apply=%region_6.7 | all-reduce | flops 128 | bytes 1024 | tf_op jit(solution)/shard_map/psum | solution.py:39
  244.0 10.8 %fusion.2 = bf16[8,80,4864]{2,1,0:T(8,128)(2,1)} fusion(f32[8,80,4864]{2,1,0:T(8,128)} %get-tuple-element.82, bf16[8,80,4864]{2,1,0:T(8,128)(2,1)} %get-tuple-element.81, f32[8]{0:T(128)S(1)} %get-tuple-element.36), kind=kLoop, calls=%fused_computation.8 | loop fusion | flops 12451840 | bytes 24903712 | tf_op jit(solution)/shard_map/convert_element_type | solution.py:42
  (27 shorter events, 5.5 us)
Async XLA Ops:
  7.2 12.8 %copy-start.2 = (f32[80]{0:T(128)S(1)}, f32[80]{0:T(128)}, u32[]{:S(2)}) copy-start(f32[80]{0:T(128)} %param.11) | copy-start | bytes 964
  7.2 12.8 %copy-start = (f32[4864]{0:T(1024)S(1)}, f32[4864]{0:T(1024)}, u32[]{:S(2)}) copy-start(f32[4864]{0:T(1024)} %param.12) | copy-start | bytes 58372
  7.2 88.4 %all-gather.2.cloned.1.call-start = ((), (), s32[]{:S(2)}) async-start(), calls=%async_computation | async-start | bytes 5603328 | tf_op jit(solution)/shard_map/all_gather | solution.py:12
  20.1 128.6 %copy-start.1 = (f32[512]{0:T(512)S(1)}, f32[512]{0:T(512)}, u32[]{:S(2)}) copy-start(f32[512]{0:T(512)} %param.13) | copy-start | bytes 6148
Sparse Core Ops, SparseCore 0:
  10.2 85.3 all-gather.1
